TPU v7x, 512 devices: a whole 4x4x16 slice. The times are simulated.
512 devices in a mesh: term: 64 (over z, x), sector: 8 (over y, core).
Axes of the slice: x: 4, y: 4, z: 16, core: 2. Of those that a mesh axis runs over, the one named last changes fastest.
Arguments:
- wave_blocks: bfloat16 [16, 512, 512], P(None, 'term'), may hold values from -0.59765625 to 0.59765625
- left_ops: bfloat16 [8, 128, 512, 512], P('sector', 'term'), may hold values from -0.25 to 0.25
- right_ops: bfloat16 [8, 256, 512, 512], P('sector', 'term'), may hold values from -0.25 to 0.25
- wanted: int32 [8, 64, 2], P('sector'), may hold values from 0 to 15, as said below
- pairs: int32 [8, 64, 12], P('sector', 'term'), may hold values from 0 to 15, as said below
- targets: int32 [8, 64, 12], P('sector', 'term'), may hold values from 0 to 1
- live: int32 [8, 64], P('sector', 'term'), may hold values from 1 to 12, as said below
Outputs:
- sigma: float32 [16, 512, 512], P('sector', 'term')
Inputs may be any that keep to these rules, and one draw needn't show every extreme that they name: `wanted`: the sectors listed for one section are distinct. `pairs`: codes are distinct within a section; a code c names half product c // 4 and right operator c % 4 of the section. Only the first live slots of a section are used; in every draw some section has 12 live slots.
All inputs are finite; a program needn't handle non-finite values.
Results may differ from a plain program's by a relative error of at most 0.0029.
Values may be sent and summed in bfloat16 or wider, within the bound.
A program may use at most 64 MiB of HBM per device.

v0:
```python
import jax
import jax.numpy as jnp
from jax import lax
from jax.sharding import PartitionSpec as P

SEC_DEV = 2
OPS_R = 4


def on_device(wave_blocks, left_ops, right_ops, wanted, pairs, targets, live):
    sections = lax.axis_size("term")
    section = lax.axis_index("term")
    block_size = left_ops.shape[2]
    gathered = lax.all_gather(wave_blocks, "term", axis=1, tiled=True)
    sources = lax.dynamic_index_in_dim(wanted[0], section, 0, keepdims=False)
    blocks = jnp.take(gathered, sources, axis=0)
    halves = jnp.einsum("aij,njk->anik", left_ops[0], blocks, preferred_element_type=jnp.float32)
    halves = halves.astype(jnp.bfloat16).reshape(-1, block_size, block_size)
    rights = right_ops[0]
    pair_codes = pairs[0, 0]
    slot_targets = targets[0, 0]

    def slot_step(slot, partial_value):
        pair_code = pair_codes[slot]
        half_pick = lax.dynamic_index_in_dim(halves, pair_code // OPS_R, 0, keepdims=False)
        right_pick = lax.dynamic_index_in_dim(rights, pair_code % OPS_R, 0, keepdims=False)
        product = lax.dot_general(
            half_pick, right_pick, (((1,), (1,)), ((), ())), preferred_element_type=jnp.float32
        )
        owner = slot_targets[slot]
        current = lax.dynamic_index_in_dim(partial_value, owner, 0, keepdims=False)
        return lax.dynamic_update_index_in_dim(partial_value, current + product, owner, 0)

    partial_value = jnp.zeros((SEC_DEV, block_size, block_size), jnp.float32)
    partial_value = lax.fori_loop(0, live[0, 0], slot_step, partial_value)
    summed = lax.psum(partial_value, "term")
    row_count = block_size // sections
    sigma = lax.dynamic_slice_in_dim(summed, section * row_count, row_count, 1)
    return sigma


def solution(mesh):
    return jax.shard_map(
        on_device,
        mesh=mesh,
        in_specs=(
            P(None, "term", None),
            P("sector", "term", None, None),
            P("sector", "term", None, None),
            P("sector", None, None),
            P("sector", "term", None),
            P("sector", "term", None),
            P("sector", "term"),
        ),
        out_specs=P("sector", "term", None),
        check_vma=False,
    )
```

profile of v0, /device:TPU:1, one launch (start us, length us, event | category | flops | bytes accessed | tf_op | source)
XLA Modules:
  0.0 561.5 jit_solution(3739584098331673386)
XLA Ops:
  6.5 0.7 all-gather.2.cloned.1.call-update
  7.3 0.9 dynamic-slice_reduce_fusion
  8.2 166.5 %all-gather.2.cloned.1.call-done = bf16[16,512,512]{2,1,0:T(8,128)(2,1)} async-done(((bf16[16,8,512]{2,1,0:T(8,128)(2,1)}), bf16[16,512,512]{2,1,0:T(8,128)(2,1)}) %all-gather.2.cloned.1.call-update) | async-done | bytes 8388624 | tf_op jit(solution)/shard_map/all_gather | solution.py:14
  174.7 5.0 gather_fusion
  179.7 2.7 convert_bitcast_fusion
  182.4 2.4 copy.10
  184.8 0.2 broadcast_in_dim.20
  185.0 0.4 copy-done.2
  185.4 68.8 %while.12 = (s32[]{:T(128)}, f32[2,512,512]{2,1,0:T(8,128)S(1)}, s32[]{:T(128)}, s32[12]{0:T(128)S(1)}, s32[12]{0:T(128)S(1)}, /*index=5*/bf16[4,512,512]{2,1,0:...) while((s32[]{:T(128)}, f32[2,512,512]{2,1,0:T(8,128)S(1)}, ...), condition=%wide.region_1.2_spmd, body=%wide.region_0.1_spmd.sunk | while | flops 268697632 | bytes 5243376 | solution.py:35
  186.1 0.6 dynamic_slice.61
  188.9 0.6 dynamic_slice.60
  191.2 0.1 constant_dynamic-slice_fusion.3
  191.3 1.7 fusion.19
  193.7 0.6 dynamic_slice.61
  196.5 0.6 dynamic_slice.60
  198.8 0.1 constant_dynamic-slice_fusion.3
  198.9 1.7 fusion.19
  201.2 0.6 dynamic_slice.61
  204.1 0.6 dynamic_slice.60
  206.4 0.1 constant_dynamic-slice_fusion.3
  206.5 1.7 fusion.19
  208.8 0.6 dynamic_slice.61
  211.7 0.6 dynamic_slice.60
  213.9 0.1 constant_dynamic-slice_fusion.3
  214.0 1.7 fusion.19
  216.4 0.6 dynamic_slice.61
  219.2 0.6 dynamic_slice.60
  221.5 0.1 constant_dynamic-slice_fusion.3
  221.6 1.7 fusion.19
  223.9 0.6 dynamic_slice.61
  226.8 0.6 dynamic_slice.60
  229.1 0.1 constant_dynamic-slice_fusion.3
  229.2 1.7 fusion.19
  231.5 0.6 dynamic_slice.61
  234.4 0.6 dynamic_slice.60
  236.7 0.1 constant_dynamic-slice_fusion.3
  236.7 1.7 fusion.19
  239.1 0.6 dynamic_slice.61
  241.9 0.6 dynamic_slice.60
  244.2 0.1 constant_dynamic-slice_fusion.3
  244.3 1.7 fusion.19
  246.7 0.6 dynamic_slice.61
  249.5 0.6 dynamic_slice.60
  251.8 0.1 constant_dynamic-slice_fusion.3
  251.9 1.7 fusion.19
  254.2 1.3 copy-done.1
  255.5 297.8 %all-reduce.2.cloned.1.call-done = f32[2,512,512]{2,1,0:T(8,128)} async-done(((f32[2,512,512]{2,1,0:T(8,128)}), f32[2,512,512]{2,1,0:T(8,128)}) %all-reduce.2.cloned.1.call-update) | async-done | bytes 2097168 | tf_op jit(solution)/shard_map/psum | solution.py:36
  553.3 1.4 constant_dynamic-slice_fusion.1
  (12 shorter events, 0.1 us)
Async XLA Ops:
  6.5 173.2 %copy-start = (bf16[1,2,512,512]{3,2,1,0:T(8,128)(2,1)S(1)}, bf16[1,2,512,512]{3,2,1,0:T(8,128)(2,1)}, u32[]{:S(2)}) copy-start(bf16[1,2,512,512]{3,2,1,0:T(8,128)(2,1)} %param.10) | copy-start | bytes 3145732
  6.5 168.1 %all-gather.2.cloned.1.call-start = ((), (), s32[]{:S(2)}) async-start(), calls=%async_computation | async-start | bytes 8519680 | tf_op jit(solution)/shard_map/all_gather | solution.py:14
  7.3 546.0 %all-reduce.2.cloned.1.call-start = ((), (), s32[]{:S(2)}) async-start(), calls=%async_computation.1 | async-start | bytes 4194304 | tf_op jit(solution)/shard_map/psum | solution.py:36
  184.7 0.7 copy-start.2
  184.8 0.7 copy-start.3
  254.2 1.3 copy-start.1
Sparse Core Ops, SparseCore 0:
  10.2 164.3 all-gather.1
  255.7 297.5 all-reduce.1
where the time goes:
time: 571 us; the launch traced here: 562 us
  waiting for transfers between devices  465 us (81%)
  loops' own time  42.5 us (7%)
  local copies, waits for them, and re-layouts  22.8 us (4%)
  matrix products  17.7 us (3%)
  between operations  13.5 us (2%)
    psum x1, waiting for transfers between devices, on_device(): summed = lax.psum(partial_value, 'term')  298 us
    all_gather x1, waiting for transfers between devices, on_device(): gathered = lax.all_gather(wave_blocks, 'term', axis=1, tiled=True)  166 us
    another operation x1, loops' own time, on_device(): partial_value = lax.fori_loop(0, live[0, 0], slot_step, partial_value)  42.5 us
    dot_general x9, matrix products, slot_step(): lax.dot_general(half_pick, right_pick, (((1,), (1,)), ((), ())), preferre...  15.1 us
  transfers between devices with their start and end apart: 2, of which 2 were waited for; matrix products, arithmetic and copies ran while one was open for 0% of the time, Pallas kernels for 0%

commit v1 on v0

v1 whole, which is shorter than its diff:
```python
import jax
import jax.numpy as jnp
from jax import lax
from jax.experimental import pallas as pl
from jax.experimental.pallas import tpu as pltpu
from jax.sharding import PartitionSpec as P

MESH = pl.DeviceIdType.MESH
NX, NY, NZ = 4, 4, 16
SLAB = NX * NY * 2
NZH = NZ // 2
OFFS = (2, 1, 3, 0)


def place():
    term = lax.axis_index("term")
    sector = lax.axis_index("sector")
    z, x = term // NX, lax.rem(term, NX)
    y, c = sector // 2, lax.rem(sector, 2)
    return z, x, y, c


def dev(z, x, y, c):
    return (z * NX + x, y * 2 + c)


def remote(src, dst, send, recv, target):
    return pltpu.make_async_remote_copy(
        src_ref=src, dst_ref=dst, send_sem=send, recv_sem=recv, device_id=target, device_id_type=MESH
    )


def wave_kernel(wave_ref, want_ref, w_ref, held, packed, want_v, want_s, send1, recv1, send2, recv2, sendw, recvw, local):
    z, x, y, c = place()
    sector = y * 2 + c
    barrier = pltpu.get_barrier_semaphore()

    def greet_z(d, _):
        pl.semaphore_signal(barrier, inc=1, device_id=dev(lax.rem(z + d, NZ), x, y, c), device_id_type=MESH)
        return 0

    def slab_core(e):
        return lax.rem(x + e // 8, NX), lax.rem(y + lax.rem(e, 8) // 2, NY), lax.rem(c + e, 2)

    def greet_slab(e, _):
        tx, ty, tc = slab_core(e)
        pl.semaphore_signal(barrier, inc=1, device_id=dev(z, tx, ty, tc), device_id_type=MESH)
        return 0

    lax.fori_loop(1, NZ, greet_z, 0)
    lax.fori_loop(1, SLAB, greet_slab, 0)
    pl.semaphore_wait(barrier, NZ - 1 + SLAB - 1)

    cols = pl.ds(pl.multiple_of(y * 128, 128), 128)
    zm = lax.rem(z, NZH)

    def stage1(i, there):
        tz = lax.rem(z + jnp.where(c == 0, i, NZ - i), NZ)
        fz = lax.rem(z + jnp.where(c == 0, NZ - i, i), NZ)
        slot = zm if there else lax.rem(fz, NZH)
        return remote(wave_ref.at[:, :, cols], held.at[slot], send1.at[i - 1], recv1.at[i - 1], dev(tz, x, y, c))

    def start1(i, _):
        stage1(i, True).start()
        return 0

    def wantcopy(e):
        ty, tc = lax.rem(y + e // 2, NY), lax.rem(c + e, 2)
        return remote(want_ref.at[z], want_v.at[sector], sendw.at[e], recvw.at[e], dev(z, x, ty, tc))

    for e in range(1, 8):
        wantcopy(e).start()
    lax.fori_loop(1, NZH, start1, 0)

    @pl.when(c == 0)
    def _():
        stage1(NZH, True).start()

    @pl.when(c == 1)
    def _():
        held[zm] = wave_ref[:, :, cols]

    want_v[sector] = want_ref[z]
    for e in range(1, 8):
        wantcopy(e).wait()
    copy = pltpu.make_async_copy(want_v, want_s, local)
    copy.start()
    copy.wait()

    def wait1(i, _):
        stage1(i, False).wait()
        return 0

    lax.fori_loop(1, NZH, wait1, 0)

    @pl.when(c == 0)
    def _():
        stage1(NZH, False).wait()

    def stage2(e):
        tx, ty, tc = slab_core(e)
        return remote(packed.at[e], w_ref.at[:, c, :, x, :, cols], send2.at[e], recv2.at[e], dev(z, tx, ty, tc))

    def pack(e, _):
        tx, ty, tc = slab_core(e)
        for j in range(2):
            source = want_s[ty * 2 + tc, 0, tx * 2 + j]
            packed[e, j] = held[:, source]
        stage2(e).start()
        return 0

    lax.fori_loop(1, SLAB, pack, 0)
    for j in range(2):
        source = want_s[sector, 0, x * 2 + j]
        w_ref[j, c, :, x, :, cols] = held[:, source]

    def wait2(e, _):
        stage2(e).wait()
        return 0

    lax.fori_loop(1, SLAB, wait2, 0)


def exchange_wave(wave, want):
    return pl.pallas_call(
        wave_kernel,
        out_shape=jax.ShapeDtypeStruct((2, 2, NZH, NX, 8, 512), jnp.bfloat16),
        in_specs=[pl.BlockSpec(memory_space=pltpu.VMEM)] * 2,
        out_specs=pl.BlockSpec(memory_space=pltpu.VMEM),
        scratch_shapes=[
            pltpu.VMEM((NZH, 16, 8, 128), jnp.bfloat16),
            pltpu.VMEM((SLAB, 2, NZH, 8, 128), jnp.bfloat16),
            pltpu.VMEM((8, 1, 128), jnp.int32),
            pltpu.SMEM((8, 1, 128), jnp.int32),
            pltpu.SemaphoreType.DMA((NZH,)),
            pltpu.SemaphoreType.DMA((NZH,)),
            pltpu.SemaphoreType.DMA((SLAB,)),
            pltpu.SemaphoreType.DMA((SLAB,)),
            pltpu.SemaphoreType.DMA((8,)),
            pltpu.SemaphoreType.DMA((8,)),
            pltpu.SemaphoreType.DMA,
        ],
        compiler_params=pltpu.CompilerParams(collective_id=0, has_side_effects=True),
    )(wave, want)


def sigma_kernel(
    w_ref, l_ref, r_ref, pairs, targets, live, out_ref, lp, halves, acc, xsend, xrecv, xown, zsend, zrecv, zown,
    sendx, recvx, sendz, recvz,
):
    z, x, y, c = place()
    barrier = pltpu.get_barrier_semaphore()

    def greet_z(d, _):
        pl.semaphore_signal(barrier, inc=1, device_id=dev(lax.rem(z + d, NZ), x, y, c), device_id_type=MESH)
        return 0

    lax.fori_loop(1, NZ, greet_z, 0)
    for e in range(1, NX):
        pl.semaphore_signal(barrier, inc=1, device_id=dev(z, lax.rem(x + e, NX), y, c), device_id_type=MESH)

    zb, zm = z // NZH, lax.rem(z, NZH)
    m = lax.broadcasted_iota(jnp.int32, (512, 256), 1) // (NX * 8)
    upper = (m >= zm) == (zb == 1)
    for a in range(2):
        low, high = l_ref[a, :, :256], l_ref[a, :, 256:]
        lp[a, :, 256:] = jnp.where(upper, high, low)
        lp[a, :, :256] = jnp.where(upper, low, high)

    def x_copy(q, e):
        return remote(
            xsend.at[q, e], xrecv.at[q, e], sendx.at[q, e], recvx.at[q, e], dev(z, lax.rem(x + e, NX), y, c)
        )

    def region(q):
        return lax.rem(z // 4 + OFFS[q], 4)

    def compute(q):
        rows = pl.ds(pl.multiple_of(region(q) * 128, 128), 128)
        for a in range(2):
            left = lp[a, rows, :]
            for j in range(2):
                half = jnp.dot(left, w_ref[j], preferred_element_type=jnp.float32)
                halves[a * 2 + j] = half.astype(jnp.bfloat16)
        acc[...] = jnp.zeros_like(acc)

        def slot_step(k, _):
            code = pairs[0, 0, k]
            product = lax.dot_general(
                halves[code // 4],
                r_ref[lax.rem(code, 4)],
                (((1,), (1,)), ((), ())),
                preferred_element_type=jnp.float32,
            )
            product = product.reshape(4, NX, 8, 512)
            used = k < live[0, 0]
            for t in range(2):
                acc[t] += jnp.where(used & (targets[0, 0, k] == t), product, 0.0)
            return 0

        lax.fori_loop(0, 12, slot_step, 0)
        for t in range(2):
            xown[q, t] = acc[t, :, x]
            for e in range(1, NX):
                xsend[q, e, t] = acc[t, :, lax.rem(x + e, NX)].astype(jnp.bfloat16)

    def z_copy(q, zz):
        tz = region(q) * 4 + zz
        return tz, lambda: remote(zsend.at[q, zz], zrecv.at[z], sendz.at[q, zz], recvz.at[z], dev(tz, x, y, c))

    def finish_x(q):
        for e in range(1, NX):
            x_copy(q, e).wait()
        for zz in range(4):
            tz, make = z_copy(q, zz)
            for t in range(2):
                total = xown[q, t, zz]
                for e in range(1, NX):
                    total = total + xrecv[q, e, t, zz].astype(jnp.float32)
                zsend[q, zz, t] = total.astype(jnp.bfloat16)
                if OFFS[q] == 0:

                    @pl.when(tz == z)
                    def _():
                        zown[t] = total

            if OFFS[q] == 0:

                @pl.when(tz != z)
                def _():
                    make().start()
            else:
                make().start()

    for q in range(4):
        compute(q)
        if q == 0:
            pl.semaphore_wait(barrier, NZ - 1 + NX - 1)
        for e in range(1, NX):
            x_copy(q, e).start()
        if q > 0:
            finish_x(q - 1)
    finish_x(3)

    for q in range(4):
        for zz in range(4):
            tz, make = z_copy(q, zz)
            if OFFS[q] == 0:

                @pl.when(tz != z)
                def _():
                    make().wait_send()
            else:
                make().wait_send()

    out_ref[...] = zown[...]

    def add(d, _):
        fz = lax.rem(z + d, NZ)
        remote(zsend.at[0, 0], zrecv.at[fz], sendz.at[0, 0], recvz.at[fz], dev(fz, x, y, c)).wait_recv()
        out_ref[...] += zrecv[fz].astype(jnp.float32)
        return 0

    lax.fori_loop(1, NZ, add, 0)


def sigma_rows(w, left, right, pairs, targets, live):
    vmem = pl.BlockSpec(memory_space=pltpu.VMEM)
    smem = pl.BlockSpec(memory_space=pltpu.SMEM)
    return pl.pallas_call(
        sigma_kernel,
        out_shape=jax.ShapeDtypeStruct((2, 8, 512), jnp.float32),
        in_specs=[vmem] * 3 + [smem] * 3,
        out_specs=vmem,
        scratch_shapes=[
            pltpu.VMEM((2, 512, 512), jnp.bfloat16),
            pltpu.VMEM((4, 128, 512), jnp.bfloat16),
            pltpu.VMEM((2, 4, NX, 8, 512), jnp.float32),
            pltpu.VMEM((4, NX, 2, 4, 8, 512), jnp.bfloat16),
            pltpu.VMEM((4, NX, 2, 4, 8, 512), jnp.bfloat16),
            pltpu.VMEM((4, 2, 4, 8, 512), jnp.float32),
            pltpu.VMEM((4, 4, 2, 8, 512), jnp.bfloat16),
            pltpu.VMEM((NZ, 2, 8, 512), jnp.bfloat16),
            pltpu.VMEM((2, 8, 512), jnp.float32),
            pltpu.SemaphoreType.DMA((4, NX)),
            pltpu.SemaphoreType.DMA((4, NX)),
            pltpu.SemaphoreType.DMA((4, 4)),
            pltpu.SemaphoreType.DMA((NZ,)),
        ],
        compiler_params=pltpu.CompilerParams(collective_id=1, has_side_effects=True),
    )(w, left, right, pairs, targets, live)


def on_device(wave_blocks, left_ops, right_ops, wanted, pairs, targets, live):
    want = jnp.pad(wanted.reshape(NZ, 1, NX * 2), ((0, 0), (0, 0), (0, 128 - NX * 2)))
    w = exchange_wave(wave_blocks, want).reshape(2, 512, 512)
    return sigma_rows(w, left_ops[0], right_ops[0], pairs, targets, live)


def solution(mesh):
    return jax.shard_map(
        on_device,
        mesh=mesh,
        in_specs=(
            P(None, "term", None),
            P("sector", "term", None, None),
            P("sector", "term", None, None),
            P("sector", None, None),
            P("sector", "term", None),
            P("sector", "term", None),
            P("sector", "term"),
        ),
        out_specs=P("sector", "term", None),
        check_vma=False,
    )
```

time: 571 us -> 87.3 us (0.15); the launches traced: 562 us -> 86.5 us
  waiting for transfers between devices: 465 us -> 0 us
  Pallas kernels: 0 us -> 83 us
  loops' own time: 42.5 us -> 0 us
  local copies, waits for them, and re-layouts: 22.8 us -> 2.83 us
  matrix products: 17.7 us -> 0 us
  between operations: 13.5 us -> 0.67 us
    psum x1 -> x0, waiting for transfers between devices: 298 us -> none  [on_device(): summed = lax.psum(partial_value, 'term')]
    all_gather x1 -> x0, waiting for transfers between devices: 166 us -> none  [on_device(): gathered = lax.all_gather(wave_blocks, 'term', axis=1, tiled=True)]
    pallas_call x0 -> x2, Pallas kernels: none -> 83 us  [the longest x1 46.8 us: exchange_wave(): pl.pallas_call(wave_kernel, out_shape=jax.ShapeDtypeStruct((2, 2, NZH, NX...]
    another operation x1 -> x0, loops' own time: 42.5 us -> none  [on_device(): partial_value = lax.fori_loop(0, live[0, 0], slot_step, partial_value)]
    dot_general x10 -> x0, matrix products: 17.7 us -> none  [the longest x9 15.1 us: slot_step(): lax.dot_general(half_pick, right_pick, (((1,), (1,)), ((), ())), preferre...]
    dynamic_slice x29 -> x0, local copies, waits for them, and re-layouts: 13.4 us -> none  [the longest x9 5.26 us: slot_step(): owner = slot_targets[slot]]
  transfers between devices with their start and end apart: 2 -> 0, of which waited for: 2 -> 0; matrix products, arithmetic and copies ran while one was open for 0% -> 0% of each run, Pallas kernels for 0% -> 0%
where the time goes in v1:
time: 87.3 us; the launch traced here: 86.5 us
  Pallas kernels  83 us (95%)
  local copies, waits for them, and re-layouts  2.83 us (3%)
    pallas_call x1, Pallas kernels, exchange_wave(): pl.pallas_call(wave_kernel, out_shape=jax.ShapeDtypeStruct((2, 2, NZH, NX...  46.8 us
    pallas_call x1, Pallas kernels, sigma_rows(): pl.pallas_call(sigma_kernel, out_shape=jax.ShapeDtypeStruct((2, 8, 512),...  36.2 us
    unnamed x2, local copies, waits for them, and re-layouts  2.14 us

profile of v1, /device:TPU:1, one launch (start us, length us, event | category | flops | bytes accessed | tf_op | source)
XLA Modules:
  0.0 86.5 jit_solution(3362182524128881776)
XLA Ops:
  0.7 0.8 copy.10
  1.4 0.1 reshape.6
  1.5 0.6 pad.4.want_ref
  2.1 46.8 %shard_map.73 = bf16[2,2,8,4,8,512]{5,4,3,2,1,0:T(8,128)(2,1)} custom-call(bf16[16,8,512]{2,1,0:T(8,128)(2,1)} %wave_ref.1, s32[16,1,128]{2,1,0:T(1,128)} %pad.4.want_ref), custom_call_target="tpu_custom_call" | custom-call | tf_op jit(solution)/shard_map/pallas_call | solution.py:125
  48.9 36.2 %shard_map.74 = f32[2,8,512]{2,1,0:T(8,128)} custom-call(bf16[2,512,512]{2,1,0:T(8,128)(2,1)} %bitcast.4, bf16[2,512,512]{2,1,0:T(8,128)(2,1)} %bitcast.6, bf16[4,512,512]{2,1,0:T(8,128)(2,1)} %bitcast.5, s32[1,1,12]{2,1,0:T(1,128)} %pairs.1, s32[1,1,12]{2,1,0:T(1,128)} %targets.1, s32[1,1]{1,0:T(1,128)S(6)} %copy.13.live), custom_call_target="tpu_custom_call" | custom-call | tf_op jit(solution)/shard_map/pallas_call | solution.py:270
  85.1 1.4 %copy.14 = f32[2,8,512]{2,1,0:T(8,128)} copy(f32[2,8,512]{2,1,0:T(8,128)} %shard_map.74) | data formatting | bytes 65536

commit v2 on v0

v2 whole, which is shorter than its diff:
```python
import jax
import jax.numpy as jnp
from jax import lax
from jax.experimental import pallas as pl
from jax.experimental.pallas import tpu as pltpu
from jax.sharding import PartitionSpec as P

MESH = pl.DeviceIdType.MESH
NX, NY, NZ = 4, 4, 16
SLAB = NX * NY * 2
NZH = NZ // 2
REACH = 4
TILE = 256
GROUP = 4


def place():
    term = lax.axis_index("term")
    sector = lax.axis_index("sector")
    return term // NX, lax.rem(term, NX), sector // 2, lax.rem(sector, 2)


def dev(z, x, y, c):
    return (z * NX + x, y * 2 + c)


def remote(src, dst, send, recv, target):
    return pltpu.make_async_remote_copy(
        src_ref=src, dst_ref=dst, send_sem=send, recv_sem=recv, device_id=target, device_id_type=MESH
    )


def kernel(
    wave_ref, want_ref, l_hbm, r_hbm, pairs, targets, live, out_ref,
    left, right, lp, held1, held2, held3, held4, held5, held6, held7, held8, packed, w_parts, w, want_v, want_s, halves, acc,
    xsend, xrecv, xown, zsend, zrecv, zown,
    load, send1, recv1, send2, recv2, sendw, recvw, sendx, recvx, sendz, recvz,
):
    z, x, y, c = place()
    held = (wave_ref, held1, held2, held3, held4, held5, held6, held7, held8)
    sector = y * 2 + c
    barrier = pltpu.get_barrier_semaphore()

    def along_z(d):
        return lax.rem(z + d + NZ, NZ)

    def slab_core(e):
        return lax.rem(x + e // 8, NX), lax.rem(y + lax.rem(e, 8) // 2, NY), lax.rem(c + e, 2)

    def greet_slab(e, _):
        tx, ty, tc = slab_core(e)
        pl.semaphore_signal(barrier, inc=1, device_id=dev(z, tx, ty, tc), device_id_type=MESH)
        return 0

    for d in range(1, REACH + 1):
        for sign in (1, -1):
            pl.semaphore_signal(barrier, inc=1, device_id=dev(along_z(sign * d), x, y, c), device_id_type=MESH)
    lax.fori_loop(1, SLAB, greet_slab, 0)

    load_left = pltpu.make_async_copy(l_hbm, left, load.at[0])
    load_right = pltpu.make_async_copy(r_hbm, right, load.at[1])
    load_left.start()
    load_right.start()
    pl.semaphore_wait(barrier, 2 * REACH + SLAB - 1)

    cols = pl.ds(pl.multiple_of(y * 128, 128), 128)
    step = jnp.where(c == 0, 1, NZ - 1)

    def direct(i):
        return remote(
            wave_ref.at[:, :, cols], held[i], send1.at[i], recv1.at[i], dev(along_z(step * i), x, y, c)
        )

    def forward(i):
        return remote(
            held[i], held[i + REACH], send1.at[i + REACH], recv1.at[i + REACH],
            dev(along_z(step * REACH), x, y, c),
        )

    def want_copy(e):
        ty, tc = lax.rem(y + e // 2, NY), lax.rem(c + e, 2)
        return remote(want_ref.at[z], want_v.at[sector], sendw.at[e], recvw.at[e], dev(z, x, ty, tc))

    for e in range(1, 8):
        want_copy(e).start()
    for i in range(1, REACH + 1):
        direct(i).start()

    want_v[sector] = want_ref[z]
    for e in range(1, 8):
        want_copy(e).wait()
    want_copy_down = pltpu.make_async_copy(want_v, want_s, load.at[2])
    want_copy_down.start()
    want_copy_down.wait()

    def slab_send(u, from_z, block):
        slot = lax.rem(from_z, NZH)

        def one(e, _):
            tx, ty, tc = slab_core(e)
            for j in range(2):
                packed[u, e - 1, j] = block(want_s[ty * 2 + tc, 0, tx * 2 + j])
            remote(
                packed.at[u, e - 1], w_parts.at[:, c, slot, x, :, cols], send2, recv2, dev(z, tx, ty, tc)
            ).start()
            return 0

        lax.fori_loop(1, SLAB, one, 0)
        for j in range(2):
            w_parts[j, c, slot, x, :, cols] = block(want_s[sector, 0, x * 2 + j])

    @pl.when(c == 1)
    def _():
        slab_send(0, z, lambda source: wave_ref[source, :, cols])

    load_left.wait()
    zb, zm = z // NZH, lax.rem(z, NZH)
    upper = (lax.broadcasted_iota(jnp.int32, (512, 256), 1) // (NX * 8) >= zm) == (zb == 1)
    for a in range(2):
        low, high = left[a, :, :256], left[a, :, 256:]
        lp[a, :, 256:] = jnp.where(upper, high, low)
        lp[a, :, :256] = jnp.where(upper, low, high)

    for i in range(1, NZH + 1):
        direct(i).wait_recv()
        if i <= REACH:
            forward(i).start()
        chunk = held[i]
        if i < NZH:
            slab_send(i - 1 + c, along_z((NZ - step) * i), lambda source: chunk[source])
        else:

            @pl.when(c == 0)
            def _():
                slab_send(i - 1, along_z((NZ - step) * i), lambda source: chunk[source])

    remote(packed, packed, send2, recv2, dev(z, x, y, c)).wait()
    for i in range(1, NZH + 1):
        direct(i).wait_send()

    for j in range(2):
        w[j] = w_parts[j].astype(jnp.float32).reshape(512, 512).astype(jnp.bfloat16)
    for a in range(2):
        for j in range(2):
            for top in range(0, 512, TILE):
                half = jnp.dot(lp[a, top : top + TILE], w[j], preferred_element_type=jnp.float32)
                halves[a * 2 + j, top : top + TILE] = half.astype(jnp.bfloat16)
    load_right.wait()

    def products(h):
        acc[...] = jnp.zeros_like(acc)

        def slots(group, _):
            for top in range(0, 512, TILE):
                total = [None, None]
                for i in range(GROUP):
                    k = group * GROUP + i
                    code = pairs[0, 0, k]
                    product = lax.dot_general(
                        halves[code // 4, top : top + TILE],
                        right[lax.rem(code, 4), h * 256 : (h + 1) * 256],
                        (((1,), (1,)), ((), ())),
                        preferred_element_type=jnp.float32,
                    )
                    used = k < live[0, 0]
                    for t in range(2):
                        part = jnp.where(used & (targets[0, 0, k] == t), product, 0.0)
                        total[t] = part if i == 0 else total[t] + part
                zs = TILE // (NX * 8)
                for t in range(2):
                    acc[t, top // 32 : top // 32 + zs] += total[t].reshape(zs, NX, 8, 256)
            return 0

        lax.fori_loop(0, 12 // GROUP, slots, 0)

    def x_copy(p, e):
        return remote(
            xsend.at[p, e - 1], xrecv.at[p, e - 1], sendx.at[p, e - 1], recvx.at[p, e - 1],
            dev(z, lax.rem(x + e, NX), y, c),
        )

    def start_x(h, t):
        p = h * 2 + t
        for e in range(1, NX):
            xsend[p, e - 1] = acc[t, :, lax.rem(x + e, NX)].astype(jnp.bfloat16)
            x_copy(p, e).start()
        xown[p] = acc[t, :, x]

    def finish_x(h, t):
        p = h * 2 + t
        for e in range(1, NX):
            x_copy(p, e).wait()

        def one(d, _):
            tz = along_z(d)
            total = xown[p, tz]
            for e in range(1, NX):
                total = total + xrecv[p, e - 1, tz].astype(jnp.float32)
            zsend[p, d - 1] = total.astype(jnp.bfloat16)
            remote(zsend.at[p, d - 1], zrecv.at[p, NZ - 1 - d], sendz, recvz, dev(tz, x, y, c)).start()
            return 0

        lax.fori_loop(1, NZ, one, 0)
        total = xown[p, z]
        for e in range(1, NX):
            total = total + xrecv[p, e - 1, z].astype(jnp.float32)
        zown[t, :, h * 256 : (h + 1) * 256] = total

    products(0)
    start_x(0, 0)
    start_x(0, 1)
    products(1)
    start_x(1, 0)
    start_x(1, 1)
    for h in range(2):
        for t in range(2):
            finish_x(h, t)

    remote(zsend, zrecv, sendz, recvz, dev(z, x, y, c)).wait()
    for h in range(2):
        for t in range(2):
            total = zown[t, :, h * 256 : (h + 1) * 256]
            for d in range(NZ - 1):
                total = total + zrecv[h * 2 + t, d].astype(jnp.float32)
            out_ref[t, :, h * 256 : (h + 1) * 256] = total


def on_device(wave_blocks, left_ops, right_ops, wanted, pairs, targets, live):
    want = jnp.pad(wanted.reshape(NZ, 1, NX * 2), ((0, 0), (0, 0), (0, 128 - NX * 2)))
    vmem = pl.BlockSpec(memory_space=pltpu.VMEM)
    smem = pl.BlockSpec(memory_space=pltpu.SMEM)
    hbm = pl.BlockSpec(memory_space=pl.ANY)
    half, full, dma = jnp.bfloat16, jnp.float32, pltpu.SemaphoreType.DMA
    return pl.pallas_call(
        kernel,
        out_shape=jax.ShapeDtypeStruct((2, 8, 512), full),
        in_specs=[vmem, vmem, hbm, hbm, smem, smem, smem],
        out_specs=vmem,
        scratch_shapes=[
            pltpu.VMEM((2, 512, 512), half),
            pltpu.VMEM((4, 512, 512), half),
            pltpu.VMEM((2, 512, 512), half),
            *[pltpu.VMEM((16, 8, 128), half)] * NZH,
            pltpu.VMEM((NZH, SLAB - 1, 2, 8, 128), half),
            pltpu.VMEM((2, 2, NZH, NX, 8, 512), half),
            pltpu.VMEM((2, 512, 512), half),
            pltpu.VMEM((8, 1, 128), jnp.int32),
            pltpu.SMEM((8, 1, 128), jnp.int32),
            pltpu.VMEM((4, 512, 512), half),
            pltpu.VMEM((2, NZ, NX, 8, 256), full),
            pltpu.VMEM((4, NX - 1, NZ, 8, 256), half),
            pltpu.VMEM((4, NX - 1, NZ, 8, 256), half),
            pltpu.VMEM((4, NZ, 8, 256), full),
            pltpu.VMEM((4, NZ - 1, 8, 256), half),
            pltpu.VMEM((4, NZ - 1, 8, 256), half),
            pltpu.VMEM((2, 8, 512), full),
            dma((3,)),
            dma((NZH + 1,)),
            dma((NZH + 1,)),
            dma,
            dma,
            dma((8,)),
            dma((8,)),
            dma((4, NX - 1)),
            dma((4, NX - 1)),
            dma,
            dma,
        ],
        compiler_params=pltpu.CompilerParams(collective_id=0, has_side_effects=True),
    )(wave_blocks, want, left_ops[0], right_ops[0], pairs, targets, live)


def solution(mesh):
    return jax.shard_map(
        on_device,
        mesh=mesh,
        in_specs=(
            P(None, "term", None),
            P("sector", "term", None, None),
            P("sector", "term", None, None),
            P("sector", None, None),
            P("sector", "term", None),
            P("sector", "term", None),
            P("sector", "term"),
        ),
        out_specs=P("sector", "term", None),
        check_vma=False,
    )
```

time: 571 us -> 67.1 us (0.12); the launches traced: 562 us -> 66.9 us
  waiting for transfers between devices: 465 us -> 0 us
  Pallas kernels: 0 us -> 63.4 us
  loops' own time: 42.5 us -> 0 us
  local copies, waits for them, and re-layouts: 22.8 us -> 2.83 us
  matrix products: 17.7 us -> 0 us
  between operations: 13.5 us -> 0.66 us
    psum x1 -> x0, waiting for transfers between devices: 298 us -> none  [on_device(): summed = lax.psum(partial_value, 'term')]
    all_gather x1 -> x0, waiting for transfers between devices: 166 us -> none  [on_device(): gathered = lax.all_gather(wave_blocks, 'term', axis=1, tiled=True)]
    pallas_call x0 -> x1, Pallas kernels: none -> 63.4 us  [on_device(): pl.pallas_call(kernel, out_shape=jax.ShapeDtypeStruct((2, 8, 512), full),...]
    another operation x1 -> x0, loops' own time: 42.5 us -> none  [on_device(): partial_value = lax.fori_loop(0, live[0, 0], slot_step, partial_value)]
    dot_general x10 -> x0, matrix products: 17.7 us -> none  [the longest x9 15.1 us: slot_step(): lax.dot_general(half_pick, right_pick, (((1,), (1,)), ((), ())), preferre...]
    dynamic_slice x29 -> x0, local copies, waits for them, and re-layouts: 13.4 us -> none  [the longest x9 5.26 us: slot_step(): owner = slot_targets[slot]]
  transfers between devices with their start and end apart: 2 -> 0, of which waited for: 2 -> 0; matrix products, arithmetic and copies ran while one was open for 0% -> 0% of each run, Pallas kernels for 0% -> 0%
where the time goes in v2:
time: 67.1 us; the launch traced here: 66.9 us
  Pallas kernels  63.4 us (94%)
  local copies, waits for them, and re-layouts  2.83 us (4%)
    pallas_call x1, Pallas kernels, on_device(): pl.pallas_call(kernel, out_shape=jax.ShapeDtypeStruct((2, 8, 512), full),...  63.4 us
    unnamed x2, local copies, waits for them, and re-layouts  2.14 us

profile of v2, /device:TPU:1, one launch (start us, length us, event | category | flops | bytes accessed | tf_op | source)
XLA Modules:
  0.0 66.9 jit_solution(6477891533289888161)
XLA Ops:
  0.7 0.8 %copy.10 = s32[1,64,2]{2,1,0:T(8,128)S(1)} copy(s32[1,64,2]{1,2,0:T(2,128)} %param.10) | data formatting | bytes 1024 | tf_op args[3]
  1.4 0.1 reshape.3
  1.5 0.6 pad.4.want_ref
  2.1 63.4 %shard_map.73 = f32[2,8,512]{2,1,0:T(8,128)} custom-call(bf16[16,8,512]{2,1,0:T(8,128)(2,1)} %wave_ref.1, s32[16,1,128]{2,1,0:T(1,128)} %pad.4.want_ref, bf16[2,512,512]{2,1,0:T(8,128)(2,1)} %bitcast.4, bf16[4,512,512]{2,1,0:T(8,128)(2,1)} %bitcast.3, s32[1,1,12]{2,1,0:T(1,128)} %pairs.1, s32[1,1,12]{2,1,0:T(1,128)} %targets.1, s32[1,1]{1,0:T(1,128)S(6)} %copy.13.live), custom_call_target="tpu_custom_call" | custom-call | tf_op jit(solution)/shard_map/pallas_call | solution.py:234
  65.5 1.4 %copy.14 = f32[2,8,512]{2,1,0:T(8,128)} copy(f32[2,8,512]{2,1,0:T(8,128)} %shard_map.73) | data formatting | bytes 65536

commit v3 on v0

v3 whole, which is shorter than its diff:
```python
import jax
import jax.numpy as jnp
from jax import lax
from jax.experimental import pallas as pl
from jax.experimental.pallas import tpu as pltpu
from jax.sharding import PartitionSpec as P

MESH = pl.DeviceIdType.MESH
NX, NY, NZ = 4, 4, 16
NZH = NZ // 2
SLAB = NX * NY * 2
REACH = 3
TAIL = 2
SPREAD = NZH - TAIL
TILE = 256
GROUP = 4


def place():
    term = lax.axis_index("term")
    sector = lax.axis_index("sector")
    return term // NX, lax.rem(term, NX), sector // 2, lax.rem(sector, 2)


def dev(z, x, y, c):
    return (z * NX + x, y * 2 + c)


def remote(src, dst, send, recv, target):
    return pltpu.make_async_remote_copy(
        src_ref=src, dst_ref=dst, send_sem=send, recv_sem=recv, device_id=target, device_id_type=MESH
    )


def kernel(
    wave_ref, want_ref, l_hbm, r_hbm, pairs, targets, live, out_ref,
    left, right, lp, held, rows0, rows1, rows2, rows3, rows4, rows5, packed, late0, late1, late_packed, w_parts, w, want_v, want_s,
    halves, far_acc, near_acc, xsend, xrecv, xown, near_xsend, near_xrecv, near_xown,
    far_send, far_recv, mid_send, mid_recv, near_send, near_recv, zown,
    load, send1, recv1, send2, recv2, send3, recv3, send4, recv4, sendw, recvw, sendx, recvx, sendf, recvf, sendm, recvm,
    sendn, recvn,
):
    z, x, y, c = place()
    zb, zm = z // NZH, lax.rem(z, NZH)
    rows = (rows0, rows1, rows2, rows3, rows4, rows5)
    late = (late0, late1,)
    sector = y * 2 + c
    barrier = pltpu.get_barrier_semaphore()

    def along_z(d):
        return dev(lax.rem(z + d + NZ, NZ), x, y, c)

    def along_x(e):
        return dev(z, lax.rem(x + e, NX), y, c)

    def chip_core(e):
        return lax.rem(y + e // 2, NY), lax.rem(c + e, 2)

    def along_yc(e):
        return dev(z, x, *chip_core(e))

    greeted = [along_z(sign * d) for d in range(1, REACH + 1) for sign in (1, -1)]
    greeted += [along_x(e) for e in range(1, NX)] + [along_yc(e) for e in range(1, 8)]
    for target in greeted:
        pl.semaphore_signal(barrier, inc=1, device_id=target, device_id_type=MESH)
    load_left = pltpu.make_async_copy(l_hbm, left, load.at[0])
    load_right = pltpu.make_async_copy(r_hbm, right, load.at[1])
    load_left.start()
    load_right.start()
    pl.semaphore_wait(barrier, len(greeted))

    cols = pl.ds(pl.multiple_of(y * 128, 128), 128)
    step = jnp.where(c == 0, 1, NZ - 1)

    def direct(i):
        return remote(wave_ref.at[:, :, cols], held.at[i - 1 + c], send1.at[i], recv1.at[i], along_z(step * i))

    def forward(u):
        i = u + 1 - c
        return remote(
            held.at[u], held.at[u + REACH], send1.at[i + REACH], recv1.at[i + REACH], along_z(step * REACH)
        )

    def spread(u, e):
        return remote(held.at[u], rows[u].at[x], send2.at[u, e - 1], recv2.at[u, e - 1], along_x(e))

    def want_copy(e):
        return remote(want_ref.at[0], want_v.at[sector], sendw.at[e], recvw.at[e], along_yc(e))

    for i in range(1, REACH + 1):
        direct(i).start()
    for e in range(1, 8):
        want_copy(e).start()

    def take(u):
        if u == 0:

            @pl.when(c == 1)
            def _():
                held[0] = wave_ref[:, :, cols]

            @pl.when(c == 0)
            def _():
                direct(1).wait_recv()
        else:
            direct(u + 1 - c).wait_recv()
        if u <= NZH - REACH:

            @pl.when((u + 1 - c >= 1) & (u + 1 - c <= NZH - REACH))
            def _():
                forward(u).start()

        if u >= SPREAD:
            late[u - SPREAD][...] = held[u]
            return
        for e in range(1, NX):
            spread(u, e).start()
        rows[u][x] = held[u]

    def select(u):
        for e in range(1, NX):
            spread(u, e).wait_recv()

        def one(e, _):
            ty, tc = chip_core(e)
            for j in range(2):
                packed[u, e - 1, j] = rows[u][:, want_s[ty * 2 + tc, j, z * NX + x]]
            remote(packed.at[u, e - 1], w_parts.at[:, c, u, :, :, cols], send3, recv3, along_yc(e)).start()
            return 0

        lax.fori_loop(1, 8, one, 0)
        for j in range(2):
            w_parts[j, c, u, :, :, cols] = rows[u][:, want_s[sector, j, z * NX + x]]

    def select_late(u):
        chunk, n = late[u - SPREAD], u - SPREAD

        def one(e, _):
            k = lax.rem(e + SLAB // 2 + 4, SLAB)
            tx = lax.rem(x + k // 8, NX)
            ty, tc = chip_core(lax.rem(k, 8))

            @pl.when(k > 0)
            def _():
                for j in range(2):
                    late_packed[n, k - 1, j] = chunk[want_s[ty * 2 + tc, j, z * NX + tx]]
                remote(
                    late_packed.at[n, k - 1], w_parts.at[:, c, u, x, :, cols], send4, recv4, dev(z, tx, ty, tc)
                ).start()

            return 0

        lax.fori_loop(0, SLAB, one, 0)
        for j in range(2):
            w_parts[j, c, u, x, :, cols] = chunk[want_s[sector, j, z * NX + x]]

    take(0)
    want_v[sector] = want_ref[0]

    take(1)
    for e in range(1, 8):
        want_copy(e).wait()
    want_down = pltpu.make_async_copy(want_v, want_s, load.at[2])
    want_down.start()
    take(2)
    want_down.wait()
    select(0)
    for u in range(3, NZH):
        take(u)
        if u >= SPREAD:
            select_late(u)
        if u - 2 < SPREAD:
            select(u - 2)
    for u in range(NZH - 2, SPREAD):
        select(u)

    load_left.wait()
    source = lax.broadcasted_iota(jnp.int32, (512, 512), 0)
    column = lax.broadcasted_iota(jnp.int32, (512, 512), 1)
    u_of = lax.rem(column, 256) // 32
    from_z = jnp.where(column < 256, z + NZ - 1 - u_of, z + u_of)
    wanted_row = lax.rem(from_z, NZ) * 32 + lax.rem(column, 32)
    pick = jnp.where(source == wanted_row, 1.0, 0.0).astype(jnp.bfloat16)
    for a in range(2):
        lp[a] = jnp.dot(left[a], pick, preferred_element_type=jnp.float32).astype(jnp.bfloat16)

    @pl.when(c == 1)
    def _():
        direct(NZH).wait_recv()

    for i in range(1, NZH + 1):
        direct(i).wait_send()
    for u in range(SPREAD):
        for e in range(1, NX):
            spread(u, e).wait_send()
    load_right.wait()
    remote(packed, packed, send3, recv3, along_yc(1)).wait()
    remote(late_packed, late_packed, send4, recv4, along_yc(1)).wait()

    for j in range(2):
        w[j] = w_parts[j].astype(jnp.float32).reshape(512, 512).astype(jnp.bfloat16)

    def half_rows(b):
        return pl.ds(pl.multiple_of(b * TILE, TILE), TILE)

    for a in range(2):
        for j in range(2):
            for top in range(0, 512, TILE):
                half = jnp.dot(lp[a, top : top + TILE], w[j], preferred_element_type=jnp.float32)
                halves[a * 2 + j, top : top + TILE] = half.astype(jnp.bfloat16)

    quarter, zl = z // 4, lax.rem(z, 4)
    sibling = 2 * zb + 1 - lax.rem(quarter, 2)

    def products(p):
        near = p >= 2
        rows_of = pl.ds(pl.multiple_of((sibling if p == 2 else quarter) * 128, 128), 128) if near else half_rows(1 - zb)
        first, last = (0, 512) if near else (p * 256, p * 256 + 256)
        acc = near_acc if near else far_acc
        acc[...] = jnp.zeros_like(acc)

        def slots(group, _):
            total = [None, None]
            for i in range(GROUP):
                k = group * GROUP + i
                code = pairs[0, 0, k]
                product = lax.dot_general(
                    halves[code // 4, rows_of],
                    right[lax.rem(code, 4), first:last],
                    (((1,), (1,)), ((), ())),
                    preferred_element_type=jnp.float32,
                )
                used = k < live[0, 0]
                for t in range(2):
                    part = jnp.where(used & (targets[0, 0, k] == t), product, 0.0)
                    total[t] = part if i == 0 else total[t] + part
            for t in range(2):
                acc[t] += total[t].reshape(acc.shape[1:])
            return 0

        lax.fori_loop(0, 12 // GROUP, slots, 0)

    def x_buffers(p):
        return (near_xsend, near_xrecv, near_xown, near_acc, p - 2) if p >= 2 else (xsend, xrecv, xown, far_acc, p)

    def x_copy(p, e):
        sent, received, _, _, i = x_buffers(p)
        return remote(
            sent.at[i, e - 1], received.at[i, e - 1], sendx.at[p, e - 1], recvx.at[p, e - 1], along_x(e)
        )

    def start_x(p):
        sent, _, own, acc, i = x_buffers(p)
        for e in range(1, NX):
            for t in range(2):
                sent[i, e - 1, t] = acc[t, :, lax.rem(x + e, NX)].astype(jnp.bfloat16)
            x_copy(p, e).start()
        for t in range(2):
            own[i, t] = acc[t, :, x]

    def summed(p, t, zz):
        _, received, own, _, i = x_buffers(p)
        total = own[i, t, zz]
        for e in range(1, NX):
            total = total + received[i, e - 1, t, zz].astype(jnp.float32)
        return total

    def finish_x(p):
        for e in range(1, NX):
            x_copy(p, e).wait()

        def far(zz, _):
            for t in range(2):
                far_send[p, zz, t] = summed(p, t, zz).astype(jnp.bfloat16)
            remote(
                far_send.at[p, zz], far_recv.at[p, zm], sendf, recvf, dev((1 - zb) * NZH + zz, x, y, c)
            ).start()
            return 0

        def next_to(zz, _):
            for t in range(2):
                mid_send[zz, t] = summed(p, t, zz).astype(jnp.bfloat16)
            remote(mid_send.at[zz], mid_recv.at[zl], sendm, recvm, dev(sibling * 4 + zz, x, y, c)).start()
            return 0

        def near(d, _):
            zz = lax.rem(zl + d, 4)
            for t in range(2):
                near_send[d - 1, t] = summed(p, t, zz).astype(jnp.bfloat16)
            remote(
                near_send.at[d - 1], near_recv.at[3 - d], sendn, recvn, dev(quarter * 4 + zz, x, y, c)
            ).start()
            return 0

        if p < 2:
            lax.fori_loop(0, NZH, far, 0)
        elif p == 2:
            lax.fori_loop(0, 4, next_to, 0)
        else:
            lax.fori_loop(1, 4, near, 0)
            for t in range(2):
                zown[t] = summed(p, t, zl)

    for p in range(4):
        products(p)
        start_x(p)
        if p >= 2:
            finish_x(p - 2)
    finish_x(2)
    finish_x(3)

    remote(far_send, far_recv, sendf, recvf, along_yc(1)).wait()
    for h in range(2):
        part = slice(h * 256, h * 256 + 256)
        for t in range(2):
            total = zown[t, :, part]
            for d in range(NZH):
                total = total + far_recv[h, d, t].astype(jnp.float32)
            zown[t, :, part] = total
    remote(mid_send, mid_recv, sendm, recvm, along_yc(1)).wait()
    remote(near_send, near_recv, sendn, recvn, along_yc(1)).wait()
    for t in range(2):
        total = zown[t]
        for d in range(4):
            total = total + mid_recv[d, t].astype(jnp.float32)
        for d in range(3):
            total = total + near_recv[d, t].astype(jnp.float32)
        out_ref[t] = total


def on_device(wave_blocks, left_ops, right_ops, wanted, pairs, targets, live):
    want = jnp.swapaxes(wanted, 1, 2)
    vmem = pl.BlockSpec(memory_space=pltpu.VMEM)
    smem = pl.BlockSpec(memory_space=pltpu.SMEM)
    hbm = pl.BlockSpec(memory_space=pl.ANY)
    half, full, dma = jnp.bfloat16, jnp.float32, pltpu.SemaphoreType.DMA
    return pl.pallas_call(
        kernel,
        out_shape=jax.ShapeDtypeStruct((2, 8, 512), full),
        in_specs=[vmem, vmem, hbm, hbm, smem, smem, smem],
        out_specs=vmem,
        scratch_shapes=[
            pltpu.VMEM((2, 512, 512), half),
            pltpu.VMEM((4, 512, 512), half),
            pltpu.VMEM((2, 512, 512), half),
            pltpu.VMEM((NZH + 1, 16, 8, 128), half),
            *[pltpu.VMEM((NX, 16, 8, 128), half)] * SPREAD,
            pltpu.VMEM((SPREAD, 7, 2, NX, 8, 128), half),
            *[pltpu.VMEM((16, 8, 128), half)] * TAIL,
            pltpu.VMEM((TAIL, SLAB - 1, 2, 8, 128), half),
            pltpu.VMEM((2, 2, NZH, NX, 8, 512), half),
            pltpu.VMEM((2, 512, 512), half),
            pltpu.VMEM((8, 2, 64), jnp.int32),
            pltpu.SMEM((8, 2, 64), jnp.int32),
            pltpu.VMEM((4, 512, 512), half),
            pltpu.VMEM((2, NZH, NX, 8, 256), full),
            pltpu.VMEM((2, 4, NX, 8, 512), full),
            pltpu.VMEM((2, NX - 1, 2, NZH, 8, 256), half),
            pltpu.VMEM((2, NX - 1, 2, NZH, 8, 256), half),
            pltpu.VMEM((2, 2, NZH, 8, 256), full),
            pltpu.VMEM((2, NX - 1, 2, 4, 8, 512), half),
            pltpu.VMEM((2, NX - 1, 2, 4, 8, 512), half),
            pltpu.VMEM((2, 2, 4, 8, 512), full),
            pltpu.VMEM((2, NZH, 2, 8, 256), half),
            pltpu.VMEM((2, NZH, 2, 8, 256), half),
            pltpu.VMEM((4, 2, 8, 512), half),
            pltpu.VMEM((4, 2, 8, 512), half),
            pltpu.VMEM((3, 2, 8, 512), half),
            pltpu.VMEM((3, 2, 8, 512), half),
            pltpu.VMEM((2, 8, 512), full),
            dma((3,)),
            dma((NZH + 1,)),
            dma((NZH + 1,)),
            dma((SPREAD, NX - 1)),
            dma((SPREAD, NX - 1)),
            dma,
            dma,
            dma,
            dma,
            dma((8,)),
            dma((8,)),
            dma((4, NX - 1)),
            dma((4, NX - 1)),
            dma,
            dma,
            dma,
            dma,
            dma,
            dma,
        ],
        compiler_params=pltpu.CompilerParams(collective_id=0, has_side_effects=True),
    )(wave_blocks, want, left_ops[0], right_ops[0], pairs, targets, live)


def solution(mesh):
    return jax.shard_map(
        on_device,
        mesh=mesh,
        in_specs=(
            P(None, "term", None),
            P("sector", "term", None, None),
            P("sector", "term", None, None),
            P("sector", None, None),
            P("sector", "term", None),
            P("sector", "term", None),
            P("sector", "term"),
        ),
        out_specs=P("sector", "term", None),
        check_vma=False,
    )
```

time: 571 us -> 61.4 us (0.11)
  the two profiles are of different devices: /device:TPU:1 before, /device:TPU:32 now
where the time goes in v3:
time: 61.4 us; the launch traced here: 61.2 us
  Pallas kernels  59.2 us (96%)
  local copies, waits for them, and re-layouts  1.38 us (2%)
  between operations  0.66 us (1%)
    pallas_call x1, Pallas kernels, on_device(): pl.pallas_call(kernel, out_shape=jax.ShapeDtypeStruct((2, 8, 512), full),...  59.2 us
    unnamed x1, local copies, waits for them, and re-layouts  1.38 us

profile of v3, /device:TPU:32, one launch (start us, length us, event | category | flops | bytes accessed | tf_op | source)
XLA Modules:
  0.0 61.2 jit_solution(6293612722614548673)
XLA Ops:
  0.7 59.2 %shard_map.73 = f32[2,8,512]{2,1,0:T(8,128)} custom-call(bf16[16,8,512]{2,1,0:T(8,128)(2,1)} %wave_ref.1, s32[1,2,64]{2,1,0:T(2,128)} %bitcast.5, bf16[2,512,512]{2,1,0:T(8,128)(2,1)} %bitcast.4, bf16[4,512,512]{2,1,0:T(8,128)(2,1)} %bitcast.3, s32[1,1,12]{2,1,0:T(1,128)} %pairs.1, s32[1,1,12]{2,1,0:T(1,128)} %targets.1, s32[1,1]{1,0:T(1,128)S(6)} %copy.9.live), custom_call_target="tpu_custom_call" | custom-call | tf_op jit(solution)/shard_map/pallas_call | solution.py:337
  59.8 1.4 %copy.10 = f32[2,8,512]{2,1,0:T(8,128)} copy(f32[2,8,512]{2,1,0:T(8,128)} %shard_map.73) | data formatting | bytes 65536

commit v4 on v3

--- a/solution.py
+++ b/solution.py
@@ -13,6 +13,7 @@
 TAIL = 2
 SPREAD = NZH - TAIL
 TILE = 256
+ORDER = (8, 9, 7, 10, 6, 11, 5, 4, -4, 3, -3, 2, 0, 1, -1, -2)
 GROUP = 4
 
 
@@ -41,7 +42,6 @@
     sendn, recvn,
 ):
     z, x, y, c = place()
-    zb, zm = z // NZH, lax.rem(z, NZH)
     rows = (rows0, rows1, rows2, rows3, rows4, rows5)
     late = (late0, late1,)
     sector = y * 2 + c
@@ -63,9 +63,10 @@
     greeted += [along_x(e) for e in range(1, NX)] + [along_yc(e) for e in range(1, 8)]
     for target in greeted:
         pl.semaphore_signal(barrier, inc=1, device_id=target, device_id_type=MESH)
-    load_left = pltpu.make_async_copy(l_hbm, left, load.at[0])
     load_right = pltpu.make_async_copy(r_hbm, right, load.at[1])
-    load_left.start()
+    for k, d in enumerate(ORDER):
+        taken = pl.ds(pl.multiple_of(lax.rem(z + d + NZ, NZ) * 32, 32), 32)
+        pltpu.make_async_copy(l_hbm.at[:, taken, :], left.at[:, k * 32 : k * 32 + 32, :], load.at[0]).start()
     load_right.start()
     pl.semaphore_wait(barrier, len(greeted))
 
@@ -174,7 +175,7 @@
     for u in range(NZH - 2, SPREAD):
         select(u)
 
-    load_left.wait()
+    pltpu.make_async_copy(l_hbm, left, load.at[0]).wait()
     source = lax.broadcasted_iota(jnp.int32, (512, 512), 0)
     column = lax.broadcasted_iota(jnp.int32, (512, 512), 1)
     u_of = lax.rem(column, 256) // 32
@@ -200,21 +201,15 @@
     for j in range(2):
         w[j] = w_parts[j].astype(jnp.float32).reshape(512, 512).astype(jnp.bfloat16)
 
-    def half_rows(b):
-        return pl.ds(pl.multiple_of(b * TILE, TILE), TILE)
-
     for a in range(2):
         for j in range(2):
             for top in range(0, 512, TILE):
                 half = jnp.dot(lp[a, top : top + TILE], w[j], preferred_element_type=jnp.float32)
                 halves[a * 2 + j, top : top + TILE] = half.astype(jnp.bfloat16)
 
-    quarter, zl = z // 4, lax.rem(z, 4)
-    sibling = 2 * zb + 1 - lax.rem(quarter, 2)
-
     def products(p):
         near = p >= 2
-        rows_of = pl.ds(pl.multiple_of((sibling if p == 2 else quarter) * 128, 128), 128) if near else half_rows(1 - zb)
+        top, bottom = (p * 128, p * 128 + 128) if near else (0, 256)
         first, last = (0, 512) if near else (p * 256, p * 256 + 256)
         acc = near_acc if near else far_acc
         acc[...] = jnp.zeros_like(acc)
@@ -225,7 +220,7 @@
                 k = group * GROUP + i
                 code = pairs[0, 0, k]
                 product = lax.dot_general(
-                    halves[code // 4, rows_of],
+                    halves[code // 4, top:bottom],
                     right[lax.rem(code, 4), first:last],
                     (((1,), (1,)), ((), ())),
                     preferred_element_type=jnp.float32,
@@ -243,71 +238,49 @@
     def x_buffers(p):
         return (near_xsend, near_xrecv, near_xown, near_acc, p - 2) if p >= 2 else (xsend, xrecv, xown, far_acc, p)
 
-    def x_copy(p, e):
+    def x_copy(p, t, e):
         sent, received, _, _, i = x_buffers(p)
         return remote(
-            sent.at[i, e - 1], received.at[i, e - 1], sendx.at[p, e - 1], recvx.at[p, e - 1], along_x(e)
+            sent.at[i, e - 1, t], received.at[i, e - 1, t], sendx.at[p, t, e - 1], recvx.at[p, t, e - 1], along_x(e)
         )
 
     def start_x(p):
         sent, _, own, acc, i = x_buffers(p)
+        for t in range(2):
+            for e in range(1, NX):
+                sent[i, e - 1, t] = acc[t, :, lax.rem(x + e, NX)].astype(jnp.bfloat16)
+                x_copy(p, t, e).start()
+            own[i, t] = acc[t, :, x]
+
+    def finish_x(p, t):
+        _, received, own, _, i = x_buffers(p)
         for e in range(1, NX):
-            for t in range(2):
-                sent[i, e - 1, t] = acc[t, :, lax.rem(x + e, NX)].astype(jnp.bfloat16)
-            x_copy(p, e).start()
-        for t in range(2):
-            own[i, t] = acc[t, :, x]
-
-    def summed(p, t, zz):
-        _, received, own, _, i = x_buffers(p)
-        total = own[i, t, zz]
-        for e in range(1, NX):
-            total = total + received[i, e - 1, t, zz].astype(jnp.float32)
-        return total
-
-    def finish_x(p):
-        for e in range(1, NX):
-            x_copy(p, e).wait()
-
-        def far(zz, _):
-            for t in range(2):
-                far_send[p, zz, t] = summed(p, t, zz).astype(jnp.bfloat16)
-            remote(
-                far_send.at[p, zz], far_recv.at[p, zm], sendf, recvf, dev((1 - zb) * NZH + zz, x, y, c)
-            ).start()
-            return 0
-
-        def next_to(zz, _):
-            for t in range(2):
-                mid_send[zz, t] = summed(p, t, zz).astype(jnp.bfloat16)
-            remote(mid_send.at[zz], mid_recv.at[zl], sendm, recvm, dev(sibling * 4 + zz, x, y, c)).start()
-            return 0
-
-        def near(d, _):
-            zz = lax.rem(zl + d, 4)
-            for t in range(2):
-                near_send[d - 1, t] = summed(p, t, zz).astype(jnp.bfloat16)
-            remote(
-                near_send.at[d - 1], near_recv.at[3 - d], sendn, recvn, dev(quarter * 4 + zz, x, y, c)
-            ).start()
-            return 0
-
-        if p < 2:
-            lax.fori_loop(0, NZH, far, 0)
-        elif p == 2:
-            lax.fori_loop(0, 4, next_to, 0)
-        else:
-            lax.fori_loop(1, 4, near, 0)
-            for t in range(2):
-                zown[t] = summed(p, t, zl)
+            x_copy(p, t, e).wait()
+        for k in range(NZH if p < 2 else 4):
+            total = own[i, t, k]
+            for e in range(1, NX):
+                total = total + received[i, e - 1, t, k].astype(jnp.float32)
+            d = ORDER[k if p < 2 else p * 4 + k]
+            if d == 0:
+                zown[t] = total
+                continue
+            if p < 2:
+                sent, landed, send, recv = far_send.at[p, k, t], far_recv.at[p, k, t], sendf, recvf
+            elif p == 2:
+                sent, landed, send, recv = mid_send.at[k, t], mid_recv.at[k, t], sendm, recvm
+            else:
+                sent, landed, send, recv = near_send.at[k - 1, t], near_recv.at[k - 1, t], sendn, recvn
+            sent[...] = total.astype(jnp.bfloat16)
+            remote(sent, landed, send, recv, along_z(d)).start()
 
     for p in range(4):
         products(p)
         start_x(p)
-        if p >= 2:
-            finish_x(p - 2)
-    finish_x(2)
-    finish_x(3)
+        if p >= 1:
+            finish_x(p - 1, 0)
+            finish_x(p - 1, 1)
+    finish_x(3, 0)
+    finish_x(3, 1)
 
     remote(far_send, far_recv, sendf, recvf, along_yc(1)).wait()
     for h in range(2):
@@ -379,8 +352,8 @@
             dma,
             dma((8,)),
             dma((8,)),
-            dma((4, NX - 1)),
-            dma((4, NX - 1)),
+            dma((4, 2, NX - 1)),
+            dma((4, 2, NX - 1)),
             dma,
             dma,
             dma,

time: 61.4 us -> 60.9 us (level)
  the two profiles are of different devices: /device:TPU:32 before, /device:TPU:1 now
where the time goes in v4:
time: 60.9 us; the launch traced here: 60.7 us
  Pallas kernels  58.6 us (96%)
  local copies, waits for them, and re-layouts  1.38 us (2%)
  between operations  0.66 us (1%)
    pallas_call x1, Pallas kernels, on_device(): pl.pallas_call(kernel, out_shape=jax.ShapeDtypeStruct((2, 8, 512), full),...  58.6 us
    unnamed x1, local copies, waits for them, and re-layouts  1.38 us

profile of v4, /device:TPU:1, one launch (start us, length us, event | category | flops | bytes accessed | tf_op | source)
XLA Modules:
  0.0 60.7 jit_solution(11196929756458393218)
XLA Ops:
  0.7 58.6 %shard_map.73 = f32[2,8,512]{2,1,0:T(8,128)} custom-call(bf16[16,8,512]{2,1,0:T(8,128)(2,1)} %wave_ref.1, s32[1,2,64]{2,1,0:T(2,128)} %bitcast.5, bf16[2,512,512]{2,1,0:T(8,128)(2,1)} %bitcast.4, bf16[4,512,512]{2,1,0:T(8,128)(2,1)} %bitcast.3, s32[1,1,12]{2,1,0:T(1,128)} %pairs.1, s32[1,1,12]{2,1,0:T(1,128)} %targets.1, s32[1,1]{1,0:T(1,128)S(6)} %copy.9.live), custom_call_target="tpu_custom_call" | custom-call | tf_op jit(solution)/shard_map/pallas_call | solution.py:310
  59.3 1.4 %copy.10 = f32[2,8,512]{2,1,0:T(8,128)} copy(f32[2,8,512]{2,1,0:T(8,128)} %shard_map.73) | data formatting | bytes 65536
